TPU v7x, 128 devices: a whole 4x4x4 slice. The times are simulated.
128 devices in a mesh: batch: 32 (over z, y_hi, x), head: 4 (over y_lo, core).
Axes of the slice: x: 4, y: 4 (y_hi: 2, y_lo: 2; y = y_hi * 2 + y_lo), z: 4, core: 2. Of those that a mesh axis runs over, the one named last changes fastest.
Arguments:
- features: bfloat16 [4096, 24, 512], P(('batch', 'head')), may hold values from -6 to 6
- state_h: bfloat16 [4096, 1024], P(('batch', 'head')), may hold values from -0.8984375 to 0.8984375
- state_c: bfloat16 [4096, 1024], P(('batch', 'head')), may hold values from -4 to 4
- valid: int32 [4096], P(('batch', 'head')), may hold values 0 or 1
- ends: int32 [4096, 24], P(('batch', 'head')), may hold values 0 or 1
- policy: int32 [4096, 1], P(('batch', 'head')), may hold values from 0 to 31; in each aligned block of 32 rows (0 to 31, 32 to 63, ...) at most 2 rows name the same one
- actions: int32 [4096, 16], P(('batch', 'head')), may hold values from 0 to 17
- w_input: bfloat16 [512, 4, 1024], P('batch', None, 'head'), may hold values from -0.25 to 0.25
- w_recur: bfloat16 [1024, 4, 1024], P('batch', None, 'head'), may hold values from -0.1875 to 0.1875
- lstm_bias: float32 [4, 1024], replicated, may hold values from -3 to 5
- w_hidden: bfloat16 [32, 1024, 1024], P('head'), may hold values from -0.1875 to 0.1875
- w_value: bfloat16 [32, 512], P('head'), may hold values from -0.25 to 0.25
- w_advantage: bfloat16 [32, 512, 18], P('head'), may hold values from -0.25 to 0.25
Outputs:
- q_values: float32 [4096, 16, 18], P(('batch', 'head'))
- q_taken: float32 [4096, 16], P(('batch', 'head'))
Inputs may be any that keep to these rules, and one draw needn't show every extreme that they name: In the rows of one device no policy appears more than 2 times, and some policy appears exactly 2 times.
All inputs are finite; a program needn't handle non-finite values. No bound on the sum of `valid` or of `ends` on one device may be relied on, other than what follows from the above.
Results may differ from a plain program's by a relative error of at most 0.007.
Values may be sent and summed in bfloat16 or wider, within the bound.
A program may use at most 128 MiB of HBM per device.

v0:
```python
import jax
import jax.numpy as jnp
from jax import lax
from jax.sharding import PartitionSpec as P

ACTIONS = 18
POLICIES = 32
CAPP = 2


def in_one_piece(arrays, axis, dim, along):
    widths = [a.shape[along] for a in arrays]
    both = jnp.concatenate(arrays, axis=along)
    filled = lax.all_gather(both, axis, axis=dim, tiled=True)
    return tuple(jnp.split(filled, [sum(widths[:k]) for k in range(1, len(widths))], axis=along))


def slot_table(owners, per_source, capacity, policies):
    count = owners.shape[0]
    sources = count // per_source
    place = jnp.arange(count, dtype=jnp.int32)
    anchor = place // per_source
    before = (
        (owners[:, None] == owners[None, :])
        & (anchor[:, None] == anchor[None, :])
        & (place[None, :] < place[:, None])
    )
    rank = jnp.sum(before.astype(jnp.int32), axis=1)
    target = owners * (sources * capacity) + anchor * capacity + rank
    total = policies * sources * capacity
    return (jnp.arange(total, dtype=jnp.int32)[:, None] == target[None, :]).astype(jnp.bfloat16)


def lstm_cell(pre_t, full_h, cell_state, keep_t, w_flat, bias, width):
    full_h = full_h * keep_t[:, None].astype(jnp.bfloat16)
    cell_state = cell_state * keep_t[:, None]
    gates = (
        pre_t
        + jnp.dot(full_h, w_flat, preferred_element_type=jnp.float32).reshape(-1, 4, width)
        + bias
    )
    cell_state = jax.nn.sigmoid(gates[:, 1]) * cell_state + jax.nn.sigmoid(gates[:, 0]) * jnp.tanh(
        gates[:, 2]
    )
    new_h = (jax.nn.sigmoid(gates[:, 3]) * jnp.tanh(cell_state)).astype(jnp.bfloat16)
    return (new_h, cell_state)


def shards(
    features,
    state_h,
    state_c,
    valid,
    ends,
    policy,
    actions,
    w_input,
    w_recur,
    lstm_bias,
    w_hidden,
    w_value,
    w_advantage,
):
    seq_dev, steps, width_e = features.shape
    width_h = state_h.shape[1]
    learn = actions.shape[1]
    burn = steps - learn
    keep_start = valid.astype(jnp.bfloat16)[:, None]
    start_h = state_h * keep_start
    start_c = state_c * keep_start
    w_in_rows, w_rec_rows = in_one_piece((w_input, w_recur), "head", 2, 0)
    feat_flat = features.transpose(1, 0, 2).reshape(-1, width_e)
    w_in_full = lax.all_gather(w_in_rows, "batch", axis=0, tiled=True).reshape(width_e, 4 * width_h)
    pre = jnp.dot(feat_flat, w_in_full, preferred_element_type=jnp.float32).reshape(
        steps, seq_dev, 4, width_h
    )
    w_flat = lax.all_gather(w_rec_rows, "batch", axis=0, tiled=True).reshape(width_h, 4 * width_h)
    keeps = 1.0 - ends.astype(jnp.float32).T

    def advance(carry, inputs):
        full_h, cell_state = carry
        pre_t, keep_t = inputs
        new_h, cell_state = lstm_cell(pre_t, full_h, cell_state, keep_t, w_flat, lstm_bias, width_h)
        return ((new_h, cell_state), new_h)

    _, outputs = lax.scan(advance, (start_h, start_c.astype(jnp.float32)), (pre, keeps))
    learned = outputs[burn:]
    table = slot_table(policy[:, 0], seq_dev, CAPP, POLICIES)
    packed = jnp.einsum("ks,tsu->ktu", table, learned, preferred_element_type=jnp.float32).astype(
        jnp.bfloat16
    )
    packed = packed.reshape(POLICIES, CAPP, learn, width_h)
    routed = lax.all_to_all(packed, "head", split_axis=0, concat_axis=1, tiled=True)
    local_heads, slots = (routed.shape[0], routed.shape[1])
    rows = routed.reshape(local_heads, slots * learn, width_h)
    mid = jnp.einsum("prh,phk->prk", rows, w_hidden, preferred_element_type=jnp.float32)
    mid = jnp.maximum(mid, 0.0).astype(jnp.bfloat16)
    branch = w_value.shape[1]
    value = jnp.einsum(
        "prk,pk->pr", mid[:, :, :branch], w_value, preferred_element_type=jnp.float32
    )
    advantage = jnp.einsum(
        "prk,pka->pra", mid[:, :, branch:], w_advantage, preferred_element_type=jnp.float32
    )
    q_local = value[:, :, None] + advantage - jnp.mean(advantage, axis=-1, keepdims=True)
    q_local = q_local.reshape(local_heads, slots, learn, ACTIONS)
    returned = lax.all_to_all(
        q_local.astype(jnp.bfloat16), "head", split_axis=1, concat_axis=0, tiled=True
    ).astype(q_local.dtype)
    own_table = slot_table(policy[:, 0], seq_dev, CAPP, POLICIES).astype(jnp.float32)
    q_values = jnp.dot(
        own_table.T,
        returned.reshape(POLICIES * CAPP, learn * ACTIONS),
        precision=lax.Precision.HIGHEST,
    ).reshape(seq_dev, learn, ACTIONS)
    chosen = actions[:, :, None] == jnp.arange(ACTIONS, dtype=jnp.int32)[None, None, :]
    q_taken = jnp.sum(jnp.where(chosen, q_values, 0.0), axis=-1)
    return (q_values, q_taken)


def solution(mesh):
    return jax.shard_map(
        shards,
        mesh=mesh,
        in_specs=(
            P(("batch", "head"), None, None),
            P(("batch", "head"), None),
            P(("batch", "head"), None),
            P(("batch", "head")),
            P(("batch", "head"), None),
            P(("batch", "head"), None),
            P(("batch", "head"), None),
            P("batch", None, "head"),
            P("batch", None, "head"),
            P(),
            P("head", None, None),
            P("head", None),
            P("head", None, None),
        ),
        out_specs=(P(("batch", "head"), None, None), P(("batch", "head"), None)),
        check_vma=False,
    )
```

profile of v0, /device:TPU:1, one launch (start us, length us, event | category | flops | bytes accessed | tf_op | source)
XLA Modules:
  0.0 450.7 jit_solution(334485971511818191)
XLA Ops:
  8.3 7.9 %all_gather.9 = bf16[48,4,1024]{2,1,0:T(4,128)(2,1)S(1)} all-gather(bf16[48,4,256]{2,1,0:T(4,128)(2,1)S(1)} %pad_maximum_fusion), channel_id=1, replica_groups=mesh['batch'=32,'head'=4] {'head'}, dimensions={2}, use_global_device_ids=true | all-gather | bytes 491520 | tf_op jit(solution)/shard_map/all_gather | solution.py:14
  18.4 79.2 %all-gather.3.cloned.1.call-done = bf16[512,4,1024]{2,1,0:T(4,128)(2,1)} async-done(((bf16[16,4,1024]{2,1,0:T(4,128)(2,1)}), bf16[512,4,1024]{2,1,0:T(4,128)(2,1)}) %all-gather.3.cloned.1.call-update) | async-done | bytes 4194320 | tf_op jit(solution)/shard_map/all_gather | solution.py:73
  102.1 6.6 %convolution_bitcast_fusion = f32[768,4096]{0,1:T(8,128)} fusion(bf16[512,4096]{1,0:T(8,128)(2,1)S(1)} %bitcast.92, bf16[768,512]{1,0:T(8,128)(2,1)S(1)} %bitcast.96), kind=kOutput, calls=%fused_computation.30 | convolution fusion | flops 3221225472 | bytes 17563648 | tf_op jit(solution)/shard_map/dot_general | solution.py:74
  108.7 12.7 %copy.47 = f32[768,4096]{1,0:T(8,128)} copy(f32[768,4096]{0,1:T(8,128)} %convolution_bitcast_fusion) | data formatting | bytes 25165824 | tf_op jit(solution)/shard_map/dot_general | solution.py:74
  121.3 15.6 %reshape.110 = f32[24,32,4,1024]{3,2,1,0:T(4,128)} reshape(f32[768,4096]{1,0:T(8,128)} %copy.47) | data formatting | bytes 25165824 | tf_op jit(solution)/shard_map/reshape | solution.py:74
  137.0 65.1 %all-gather.5.cloned.1.call-done = bf16[1024,4,1024]{2,1,0:T(4,128)(2,1)} async-done(((bf16[32,4,1024]{2,1,0:T(4,128)(2,1)}), bf16[1024,4,1024]{2,1,0:T(4,128)(2,1)}) %all-gather.5.cloned.1.call-update) | async-done | bytes 8388624 | tf_op jit(solution)/shard_map/all_gather | solution.py:77
  202.1 12.1 %copy.62 = bf16[128,8,4,1024]{3,1,2,0:T(8,128)(2,1)} copy(bf16[128,8,4,1024]{3,2,1,0:T(4,128)(2,1)} %bitcast.89) | data formatting | bytes 16777216
  214.2 173.0 %while.14 = (s32[]{:T(128)}, bf16[32,1024]{1,0:T(8,128)(2,1)S(1)}, f32[32,1024]{1,0:T(8,128)S(1)}, bf16[24,32,1024]{2,1,0:T(8,128)(2,1)}, f32[24,32,4,1024]{3,2,...) while((s32[]{:T(128)}, bf16[32,1024]{1,0:T(8,128)(2,1)S(1)}, ...), condition=%wide.region_2.3_spmd, body=%wide.region_1.2_spmd.sunk | while | flops 269221920 | bytes 12534885 | solution.py:86
  214.2 5.0 %fusion.55 = f32[32,4096]{1,0:T(8,128)S(1)} fusion(bf16[1024,4096]{1,0:T(8,128)(2,1)} %get-tuple-element.171, bf16[32,1024]{1,0:T(8,128)(2,1)S(1)} %get-tuple-element.157, bf16[32]{0:T(256)(128)(2,1)S(1)} %get-tuple-element.142), kind=kOutput, calls=%fused_computation.24.clone.1 | convolution fusion | flops 268468224 | bytes 8978496 | tf_op jit(solution)/shard_map/while/body/eval_jaxpr/dot_general | solution.py:39
  221.4 5.0 %fusion.55 = f32[32,4096]{1,0:T(8,128)S(1)} fusion(bf16[1024,4096]{1,0:T(8,128)(2,1)} %get-tuple-element.171, bf16[32,1024]{1,0:T(8,128)(2,1)S(1)} %get-tuple-element.157, bf16[32]{0:T(256)(128)(2,1)S(1)} %get-tuple-element.142), kind=kOutput, calls=%fused_computation.24.clone.1 | convolution fusion | flops 268468224 | bytes 8978496 | tf_op jit(solution)/shard_map/while/body/eval_jaxpr/dot_general | solution.py:39
  243.0 5.0 %fusion.55 = f32[32,4096]{1,0:T(8,128)S(1)} fusion(bf16[1024,4096]{1,0:T(8,128)(2,1)} %get-tuple-element.171, bf16[32,1024]{1,0:T(8,128)(2,1)S(1)} %get-tuple-element.157, bf16[32]{0:T(256)(128)(2,1)S(1)} %get-tuple-element.142), kind=kOutput, calls=%fused_computation.24.clone.1 | convolution fusion | flops 268468224 | bytes 8978496 | tf_op jit(solution)/shard_map/while/body/eval_jaxpr/dot_general | solution.py:39
  250.2 5.0 %fusion.55 = f32[32,4096]{1,0:T(8,128)S(1)} fusion(bf16[1024,4096]{1,0:T(8,128)(2,1)} %get-tuple-element.171, bf16[32,1024]{1,0:T(8,128)(2,1)S(1)} %get-tuple-element.157, bf16[32]{0:T(256)(128)(2,1)S(1)} %get-tuple-element.142), kind=kOutput, calls=%fused_computation.24.clone.1 | convolution fusion | flops 268468224 | bytes 8978496 | tf_op jit(solution)/shard_map/while/body/eval_jaxpr/dot_general | solution.py:39
  271.9 5.0 %fusion.55 = f32[32,4096]{1,0:T(8,128)S(1)} fusion(bf16[1024,4096]{1,0:T(8,128)(2,1)} %get-tuple-element.171, bf16[32,1024]{1,0:T(8,128)(2,1)S(1)} %get-tuple-element.157, bf16[32]{0:T(256)(128)(2,1)S(1)} %get-tuple-element.142), kind=kOutput, calls=%fused_computation.24.clone.1 | convolution fusion | flops 268468224 | bytes 8978496 | tf_op jit(solution)/shard_map/while/body/eval_jaxpr/dot_general | solution.py:39
  279.1 5.0 %fusion.55 = f32[32,4096]{1,0:T(8,128)S(1)} fusion(bf16[1024,4096]{1,0:T(8,128)(2,1)} %get-tuple-element.171, bf16[32,1024]{1,0:T(8,128)(2,1)S(1)} %get-tuple-element.157, bf16[32]{0:T(256)(128)(2,1)S(1)} %get-tuple-element.142), kind=kOutput, calls=%fused_computation.24.clone.1 | convolution fusion | flops 268468224 | bytes 8978496 | tf_op jit(solution)/shard_map/while/body/eval_jaxpr/dot_general | solution.py:39
  293.5 5.0 %fusion.55 = f32[32,4096]{1,0:T(8,128)S(1)} fusion(bf16[1024,4096]{1,0:T(8,128)(2,1)} %get-tuple-element.171, bf16[32,1024]{1,0:T(8,128)(2,1)S(1)} %get-tuple-element.157, bf16[32]{0:T(256)(128)(2,1)S(1)} %get-tuple-element.142), kind=kOutput, calls=%fused_computation.24.clone.1 | convolution fusion | flops 268468224 | bytes 8978496 | tf_op jit(solution)/shard_map/while/body/eval_jaxpr/dot_general | solution.py:39
  307.9 5.0 %fusion.55 = f32[32,4096]{1,0:T(8,128)S(1)} fusion(bf16[1024,4096]{1,0:T(8,128)(2,1)} %get-tuple-element.171, bf16[32,1024]{1,0:T(8,128)(2,1)S(1)} %get-tuple-element.157, bf16[32]{0:T(256)(128)(2,1)S(1)} %get-tuple-element.142), kind=kOutput, calls=%fused_computation.24.clone.1 | convolution fusion | flops 268468224 | bytes 8978496 | tf_op jit(solution)/shard_map/while/body/eval_jaxpr/dot_general | solution.py:39
  315.1 5.0 %fusion.55 = f32[32,4096]{1,0:T(8,128)S(1)} fusion(bf16[1024,4096]{1,0:T(8,128)(2,1)} %get-tuple-element.171, bf16[32,1024]{1,0:T(8,128)(2,1)S(1)} %get-tuple-element.157, bf16[32]{0:T(256)(128)(2,1)S(1)} %get-tuple-element.142), kind=kOutput, calls=%fused_computation.24.clone.1 | convolution fusion | flops 268468224 | bytes 8978496 | tf_op jit(solution)/shard_map/while/body/eval_jaxpr/dot_general | solution.py:39
  322.3 5.0 %fusion.55 = f32[32,4096]{1,0:T(8,128)S(1)} fusion(bf16[1024,4096]{1,0:T(8,128)(2,1)} %get-tuple-element.171, bf16[32,1024]{1,0:T(8,128)(2,1)S(1)} %get-tuple-element.157, bf16[32]{0:T(256)(128)(2,1)S(1)} %get-tuple-element.142), kind=kOutput, calls=%fused_computation.24.clone.1 | convolution fusion | flops 268468224 | bytes 8978496 | tf_op jit(solution)/shard_map/while/body/eval_jaxpr/dot_general | solution.py:39
  336.7 5.0 %fusion.55 = f32[32,4096]{1,0:T(8,128)S(1)} fusion(bf16[1024,4096]{1,0:T(8,128)(2,1)} %get-tuple-element.171, bf16[32,1024]{1,0:T(8,128)(2,1)S(1)} %get-tuple-element.157, bf16[32]{0:T(256)(128)(2,1)S(1)} %get-tuple-element.142), kind=kOutput, calls=%fused_computation.24.clone.1 | convolution fusion | flops 268468224 | bytes 8978496 | tf_op jit(solution)/shard_map/while/body/eval_jaxpr/dot_general | solution.py:39
  351.2 5.0 %fusion.55 = f32[32,4096]{1,0:T(8,128)S(1)} fusion(bf16[1024,4096]{1,0:T(8,128)(2,1)} %get-tuple-element.171, bf16[32,1024]{1,0:T(8,128)(2,1)S(1)} %get-tuple-element.157, bf16[32]{0:T(256)(128)(2,1)S(1)} %get-tuple-element.142), kind=kOutput, calls=%fused_computation.24.clone.1 | convolution fusion | flops 268468224 | bytes 8978496 | tf_op jit(solution)/shard_map/while/body/eval_jaxpr/dot_general | solution.py:39
  372.8 5.0 %fusion.55 = f32[32,4096]{1,0:T(8,128)S(1)} fusion(bf16[1024,4096]{1,0:T(8,128)(2,1)} %get-tuple-element.171, bf16[32,1024]{1,0:T(8,128)(2,1)S(1)} %get-tuple-element.157, bf16[32]{0:T(256)(128)(2,1)S(1)} %get-tuple-element.142), kind=kOutput, calls=%fused_computation.24.clone.1 | convolution fusion | flops 268468224 | bytes 8978496 | tf_op jit(solution)/shard_map/while/body/eval_jaxpr/dot_general | solution.py:39
  395.2 28.5 %all_to_all.30 = bf16[32,2,16,1024]{3,1,2,0:T(2,128)(2,1)S(1)} all-to-all(bf16[32,2,16,1024]{3,1,2,0:T(2,128)(2,1)S(1)} %copy.48), channel_id=1, replica_groups=mesh['batch'=32,'head'=4] {'head'}, dimensions={0} | all-to-all | bytes 4194304 | tf_op jit(solution)/shard_map/all_to_all | solution.py:93
  424.4 8.3 %maximum_convert_fusion = bf16[8,128,1024]{2,1,0:T(8,128)(2,1)S(1)} fusion(bf16[8,128,1024]{2,1,0:T(8,128)(2,1)S(1)} %bitcast.88, bf16[8,1024,1024]{2,1,0:T(8,128)(2,1)} %param.25), kind=kOutput, calls=%fused_computation.31 | convolution fusion | flops 2149580800 | bytes 20971520 | tf_op jit(solution)/shard_map/prh,phk->prk/dot_general | solution.py:96
  434.7 6.6 %all_to_all.31 = bf16[4,2,2304]{2,1,0:T(2,128)(2,1)S(1)} all-to-all(bf16[4,2,2304]{2,1,0:T(2,128)(2,1)S(1)} %reshape.120), channel_id=1, replica_groups=mesh['batch'=32,'head'=4] {'head'}, dimensions={0} | all-to-all | bytes 73728 | tf_op jit(solution)/shard_map/all_to_all | solution.py:107
  (161 shorter events, 129.0 us)
Async XLA Ops:
  7.2 425.5 %copy-start = (bf16[8,512,18]{1,0,2:T(8,128)(2,1)S(1)}, bf16[8,512,18]{1,0,2:T(8,128)(2,1)}, u32[]{:S(2)}) copy-start(bf16[8,512,18]{1,0,2:T(8,128)(2,1)} %param.27) | copy-start | bytes 442372
  7.2 10.6 %copy-start.1 = (bf16[32,24,512]{2,1,0:T(8,128)(2,1)S(1)}, bf16[32,24,512]{2,1,0:T(8,128)(2,1)}, u32[]{:S(2)}) copy-start(bf16[32,24,512]{2,1,0:T(8,128)(2,1)} %param.15) | copy-start | bytes 2359300
  7.2 10.9 %copy-start.9 = (s32[32]{0:T(128)S(1)}, s32[32]{0:T(128)}, u32[]{:S(2)}) copy-start(s32[32]{0:T(128)} %param.18) | copy-start | bytes 388
  7.2 10.9 %copy-start.7 = (s32[32,1]{0,1:T(1,128)S(1)}, s32[32,1]{0,1:T(1,128)}, u32[]{:S(2)}) copy-start(s32[32,1]{0,1:T(1,128)} %param.20) | copy-start | bytes 388
  7.2 11.1 %copy-start.5 = (s32[32,24]{0,1:T(8,128)S(1)}, s32[32,24]{0,1:T(8,128)}, u32[]{:S(2)}) copy-start(s32[32,24]{0,1:T(8,128)} %param.19) | copy-start | bytes 9220
  7.2 11.1 %copy-start.4 = (bf16[32,1024]{1,0:T(8,128)(2,1)S(1)}, bf16[32,1024]{1,0:T(8,128)(2,1)}, u32[]{:S(2)}) copy-start(bf16[32,1024]{1,0:T(8,128)(2,1)} %param.16) | copy-start | bytes 196612
  7.2 11.1 %copy-start.3 = (bf16[32,1024]{1,0:T(8,128)(2,1)S(1)}, bf16[32,1024]{1,0:T(8,128)(2,1)}, u32[]{:S(2)}) copy-start(bf16[32,1024]{1,0:T(8,128)(2,1)} %param.17) | copy-start | bytes 196612
  7.2 90.3 %all-gather.3.cloned.1.call-start = ((), (), s32[]{:S(2)}) async-start(), calls=%async_computation.2 | async-start | bytes 4325376 | tf_op jit(solution)/shard_map/all_gather | solution.py:73
  16.9 185.2 %all-gather.5.cloned.1.call-start = ((), (), s32[]{:S(2)}) async-start(), calls=%async_computation.3 | async-start | bytes 8650752 | tf_op jit(solution)/shard_map/all_gather | solution.py:77
  202.1 12.1 %copy-start.2 = (f32[4,1024]{1,0:T(4,128)S(1)}, f32[4,1024]{1,0:T(4,128)}, u32[]{:S(2)}) copy-start(f32[4,1024]{1,0:T(4,128)} %param.24) | copy-start | bytes 49156
  424.4 8.7 %copy-start.8 = (bf16[8,512]{1,0:T(8,128)(2,1)S(1)}, bf16[8,512]{1,0:T(8,128)(2,1)}, u32[]{:S(2)}) copy-start(bf16[8,512]{1,0:T(8,128)(2,1)} %param.26) | copy-start | bytes 24580
  433.1 9.2 %copy-start.6 = (s32[32,16]{0,1:T(8,128)S(1)}, s32[32,16]{0,1:T(8,128)}, u32[]{:S(2)}) copy-start(s32[32,16]{0,1:T(8,128)} %param.21) | copy-start | bytes 6148
Sparse Core Ops, SparseCore 0:
  17.0 80.4 all-gather.2
  100.6 101.4 all-gather.4
where the time goes:
time: 454 us; the launch traced here: 451 us
  waiting for transfers between devices  144 us (32%)
  matrix products  138 us (30%)
  local copies, waits for them, and re-layouts  82.2 us (18%)
  blocking collectives  43 us (9%)
  other arithmetic  28.7 us (6%)
  between operations  14.3 us (3%)
    dot_general x24, matrix products, lstm_cell(): jnp.dot(full_h, w_flat, preferred_element_type=jnp.float32)  119 us
    all_gather x1, waiting for transfers between devices, shards(): lax.all_gather(w_in_rows, 'batch', axis=0, tiled=True)  79.2 us
    all_gather x1, waiting for transfers between devices, shards(): lax.all_gather(w_rec_rows, 'batch', axis=0, tiled=True)  65.1 us
    all_to_all x1, blocking collectives, shards(): lax.all_to_all(packed, 'head', split_axis=0, concat_axis=1, tiled=True)  28.5 us
    dynamic_slice x24, local copies, waits for them, and re-layouts, shards(): lax.scan(advance, (start_h, start_c.astype(jnp.float32)), (pre, keeps))  26 us
    dynamic_update_slice x24, other arithmetic, shards(): lax.scan(advance, (start_h, start_c.astype(jnp.float32)), (pre, keeps))  19 us
    unnamed x26, local copies, waits for them, and re-layouts  18.5 us
    reshape x1, local copies, waits for them, and re-layouts, shards(): jnp.dot(feat_flat, w_in_full, preferred_element_type=jnp.float32)  15.6 us
  transfers between devices with their start and end apart: 2, of which 2 were waited for; matrix products, arithmetic and copies ran while one was open for 9% of the time, Pallas kernels for 0%

commit v1 on v0

--- a/solution.py
+++ b/solution.py
@@ -90,7 +90,15 @@
         jnp.bfloat16
     )
     packed = packed.reshape(POLICIES, CAPP, learn, width_h)
-    routed = lax.all_to_all(packed, "head", split_axis=0, concat_axis=1, tiled=True)
+    routed = jnp.concatenate(
+        jax.lax.all_to_all(
+            jnp.stack(jnp.split(packed, jax.lax.axis_size("head"), 0), axis=0),
+            axis_name="head",
+            split_axis=0,
+            concat_axis=0,
+        ),
+        1,
+    )
     local_heads, slots = (routed.shape[0], routed.shape[1])
     rows = routed.reshape(local_heads, slots * learn, width_h)
     mid = jnp.einsum("prh,phk->prk", rows, w_hidden, preferred_element_type=jnp.float32)

time: 454 us -> 438 us (0.965)
  other arithmetic: 28.7 us -> 17.7 us
    dynamic_update_slice x24, other arithmetic: 19 us -> 3.99 us  [shards(): lax.scan(advance, (start_h, start_c.astype(jnp.float32)), (pre, keeps))]
    unnamed x26 -> x28, local copies, waits for them, and re-layouts: 18.5 us -> 18.6 us
where the time goes in v1:
time: 438 us; the launch traced here: 436 us
  waiting for transfers between devices  144 us (33%)
  matrix products  137 us (31%)
  local copies, waits for them, and re-layouts  78.4 us (18%)
  blocking collectives  43 us (10%)
  other arithmetic  17.7 us (4%)
  between operations  14.4 us (3%)
    dot_general x24, matrix products, lstm_cell(): jnp.dot(full_h, w_flat, preferred_element_type=jnp.float32)  119 us
    all_gather x1, waiting for transfers between devices, shards(): lax.all_gather(w_in_rows, 'batch', axis=0, tiled=True)  79.2 us
    all_gather x1, waiting for transfers between devices, shards(): lax.all_gather(w_rec_rows, 'batch', axis=0, tiled=True)  65.1 us
    all_to_all x1, blocking collectives, shards(): jax.lax.all_to_all(jnp.stack(jnp.split(packed, jax.lax.axis_size('head'),...  28.5 us
    dynamic_slice x24, local copies, waits for them, and re-layouts, shards(): lax.scan(advance, (start_h, start_c.astype(jnp.float32)), (pre, keeps))  26 us
    unnamed x28, local copies, waits for them, and re-layouts  18.6 us
    reshape x1, local copies, waits for them, and re-layouts, shards(): jnp.dot(feat_flat, w_in_full, preferred_element_type=jnp.float32)  15.6 us
    dot_general x1, local copies, waits for them, and re-layouts, shards(): jnp.dot(feat_flat, w_in_full, preferred_element_type=jnp.float32)  12.7 us
  transfers between devices with their start and end apart: 2, of which 2 were waited for; matrix products, arithmetic and copies ran while one was open for 9% of the time, Pallas kernels for 0%

profile of v1, /device:TPU:1, one launch (start us, length us, event | category | flops | bytes accessed | tf_op | source)
XLA Modules:
  0.0 435.6 jit_solution(2255517060157149244)
XLA Ops:
  8.3 7.9 %all_gather.9 = bf16[48,4,1024]{2,1,0:T(4,128)(2,1)S(1)} all-gather(bf16[48,4,256]{2,1,0:T(4,128)(2,1)S(1)} %pad_maximum_fusion.1), channel_id=1, replica_groups=mesh['batch'=32,'head'=4] {'head'}, dimensions={2}, use_global_device_ids=true | all-gather | bytes 491520 | tf_op jit(solution)/shard_map/all_gather | solution.py:14
  18.4 79.2 %all-gather.3.cloned.1.call-done = bf16[512,4,1024]{2,1,0:T(4,128)(2,1)} async-done(((bf16[16,4,1024]{2,1,0:T(4,128)(2,1)}), bf16[512,4,1024]{2,1,0:T(4,128)(2,1)}) %all-gather.3.cloned.1.call-update) | async-done | bytes 4194320 | tf_op jit(solution)/shard_map/all_gather | solution.py:73
  102.1 6.6 %convolution_bitcast_fusion = f32[768,4096]{0,1:T(8,128)} fusion(bf16[512,4096]{1,0:T(8,128)(2,1)S(1)} %bitcast.96, bf16[768,512]{1,0:T(8,128)(2,1)S(1)} %bitcast.100), kind=kOutput, calls=%fused_computation.30 | convolution fusion | flops 3221225472 | bytes 17563648 | tf_op jit(solution)/shard_map/dot_general | solution.py:74
  108.7 12.7 %copy.46 = f32[768,4096]{1,0:T(8,128)} copy(f32[768,4096]{0,1:T(8,128)} %convolution_bitcast_fusion) | data formatting | bytes 25165824 | tf_op jit(solution)/shard_map/dot_general | solution.py:74
  121.4 15.6 %reshape.115 = f32[24,32,4,1024]{3,2,1,0:T(4,128)} reshape(f32[768,4096]{1,0:T(8,128)} %copy.46) | data formatting | bytes 25165824 | tf_op jit(solution)/shard_map/reshape | solution.py:74
  137.0 65.1 %all-gather.5.cloned.1.call-done = bf16[1024,4,1024]{2,1,0:T(4,128)(2,1)} async-done(((bf16[32,4,1024]{2,1,0:T(4,128)(2,1)}), bf16[1024,4,1024]{2,1,0:T(4,128)(2,1)}) %all-gather.5.cloned.1.call-update) | async-done | bytes 8388624 | tf_op jit(solution)/shard_map/all_gather | solution.py:77
  202.1 12.2 %copy.60 = bf16[128,8,4,1024]{3,1,2,0:T(8,128)(2,1)} copy(bf16[128,8,4,1024]{3,2,1,0:T(4,128)(2,1)} %bitcast.93) | data formatting | bytes 16777216
  214.3 159.0 %while.14 = (s32[]{:T(128)}, bf16[32,1024]{1,0:T(8,128)(2,1)S(1)}, f32[32,1024]{1,0:T(8,128)S(1)}, bf16[24,32,1024]{2,1,0:T(8,128)(2,1)S(1)}, f32[24,32,4,1024]{...) while((s32[]{:T(128)}, bf16[32,1024]{1,0:T(8,128)(2,1)S(1)}, ...), condition=%wide.region_2.3_spmd, body=%wide.region_1.2_spmd.sunk | while | flops 269221920 | bytes 12534761 | solution.py:86
  214.3 5.0 %fusion.56 = f32[32,4096]{1,0:T(8,128)S(1)} fusion(bf16[1024,4096]{1,0:T(8,128)(2,1)} %get-tuple-element.175, bf16[32,1024]{1,0:T(8,128)(2,1)S(1)} %get-tuple-element.161, bf16[32]{0:T(256)(128)(2,1)S(1)} %get-tuple-element.146), kind=kOutput, calls=%fused_computation.24.clone.1 | convolution fusion | flops 268468224 | bytes 8978496 | tf_op jit(solution)/shard_map/while/body/eval_jaxpr/dot_general | solution.py:39
  220.9 5.0 %fusion.56 = f32[32,4096]{1,0:T(8,128)S(1)} fusion(bf16[1024,4096]{1,0:T(8,128)(2,1)} %get-tuple-element.175, bf16[32,1024]{1,0:T(8,128)(2,1)S(1)} %get-tuple-element.161, bf16[32]{0:T(256)(128)(2,1)S(1)} %get-tuple-element.146), kind=kOutput, calls=%fused_computation.24.clone.1 | convolution fusion | flops 268468224 | bytes 8978496 | tf_op jit(solution)/shard_map/while/body/eval_jaxpr/dot_general | solution.py:39
  234.2 5.0 %fusion.56 = f32[32,4096]{1,0:T(8,128)S(1)} fusion(bf16[1024,4096]{1,0:T(8,128)(2,1)} %get-tuple-element.175, bf16[32,1024]{1,0:T(8,128)(2,1)S(1)} %get-tuple-element.161, bf16[32]{0:T(256)(128)(2,1)S(1)} %get-tuple-element.146), kind=kOutput, calls=%fused_computation.24.clone.1 | convolution fusion | flops 268468224 | bytes 8978496 | tf_op jit(solution)/shard_map/while/body/eval_jaxpr/dot_general | solution.py:39
  240.8 5.0 %fusion.56 = f32[32,4096]{1,0:T(8,128)S(1)} fusion(bf16[1024,4096]{1,0:T(8,128)(2,1)} %get-tuple-element.175, bf16[32,1024]{1,0:T(8,128)(2,1)S(1)} %get-tuple-element.161, bf16[32]{0:T(256)(128)(2,1)S(1)} %get-tuple-element.146), kind=kOutput, calls=%fused_computation.24.clone.1 | convolution fusion | flops 268468224 | bytes 8978496 | tf_op jit(solution)/shard_map/while/body/eval_jaxpr/dot_general | solution.py:39
  260.6 5.0 %fusion.56 = f32[32,4096]{1,0:T(8,128)S(1)} fusion(bf16[1024,4096]{1,0:T(8,128)(2,1)} %get-tuple-element.175, bf16[32,1024]{1,0:T(8,128)(2,1)S(1)} %get-tuple-element.161, bf16[32]{0:T(256)(128)(2,1)S(1)} %get-tuple-element.146), kind=kOutput, calls=%fused_computation.24.clone.1 | convolution fusion | flops 268468224 | bytes 8978496 | tf_op jit(solution)/shard_map/while/body/eval_jaxpr/dot_general | solution.py:39
  267.3 5.0 %fusion.56 = f32[32,4096]{1,0:T(8,128)S(1)} fusion(bf16[1024,4096]{1,0:T(8,128)(2,1)} %get-tuple-element.175, bf16[32,1024]{1,0:T(8,128)(2,1)S(1)} %get-tuple-element.161, bf16[32]{0:T(256)(128)(2,1)S(1)} %get-tuple-element.146), kind=kOutput, calls=%fused_computation.24.clone.1 | convolution fusion | flops 268468224 | bytes 8978496 | tf_op jit(solution)/shard_map/while/body/eval_jaxpr/dot_general | solution.py:39
  287.1 5.0 %fusion.56 = f32[32,4096]{1,0:T(8,128)S(1)} fusion(bf16[1024,4096]{1,0:T(8,128)(2,1)} %get-tuple-element.175, bf16[32,1024]{1,0:T(8,128)(2,1)S(1)} %get-tuple-element.161, bf16[32]{0:T(256)(128)(2,1)S(1)} %get-tuple-element.146), kind=kOutput, calls=%fused_computation.24.clone.1 | convolution fusion | flops 268468224 | bytes 8978496 | tf_op jit(solution)/shard_map/while/body/eval_jaxpr/dot_general | solution.py:39
  293.7 5.0 %fusion.56 = f32[32,4096]{1,0:T(8,128)S(1)} fusion(bf16[1024,4096]{1,0:T(8,128)(2,1)} %get-tuple-element.175, bf16[32,1024]{1,0:T(8,128)(2,1)S(1)} %get-tuple-element.161, bf16[32]{0:T(256)(128)(2,1)S(1)} %get-tuple-element.146), kind=kOutput, calls=%fused_computation.24.clone.1 | convolution fusion | flops 268468224 | bytes 8978496 | tf_op jit(solution)/shard_map/while/body/eval_jaxpr/dot_general | solution.py:39
  313.6 5.0 %fusion.56 = f32[32,4096]{1,0:T(8,128)S(1)} fusion(bf16[1024,4096]{1,0:T(8,128)(2,1)} %get-tuple-element.175, bf16[32,1024]{1,0:T(8,128)(2,1)S(1)} %get-tuple-element.161, bf16[32]{0:T(256)(128)(2,1)S(1)} %get-tuple-element.146), kind=kOutput, calls=%fused_computation.24.clone.1 | convolution fusion | flops 268468224 | bytes 8978496 | tf_op jit(solution)/shard_map/while/body/eval_jaxpr/dot_general | solution.py:39
  320.2 5.0 %fusion.56 = f32[32,4096]{1,0:T(8,128)S(1)} fusion(bf16[1024,4096]{1,0:T(8,128)(2,1)} %get-tuple-element.175, bf16[32,1024]{1,0:T(8,128)(2,1)S(1)} %get-tuple-element.161, bf16[32]{0:T(256)(128)(2,1)S(1)} %get-tuple-element.146), kind=kOutput, calls=%fused_computation.24.clone.1 | convolution fusion | flops 268468224 | bytes 8978496 | tf_op jit(solution)/shard_map/while/body/eval_jaxpr/dot_general | solution.py:39
  340.0 5.0 %fusion.56 = f32[32,4096]{1,0:T(8,128)S(1)} fusion(bf16[1024,4096]{1,0:T(8,128)(2,1)} %get-tuple-element.175, bf16[32,1024]{1,0:T(8,128)(2,1)S(1)} %get-tuple-element.161, bf16[32]{0:T(256)(128)(2,1)S(1)} %get-tuple-element.146), kind=kOutput, calls=%fused_computation.24.clone.1 | convolution fusion | flops 268468224 | bytes 8978496 | tf_op jit(solution)/shard_map/while/body/eval_jaxpr/dot_general | solution.py:39
  346.7 5.0 %fusion.56 = f32[32,4096]{1,0:T(8,128)S(1)} fusion(bf16[1024,4096]{1,0:T(8,128)(2,1)} %get-tuple-element.175, bf16[32,1024]{1,0:T(8,128)(2,1)S(1)} %get-tuple-element.161, bf16[32]{0:T(256)(128)(2,1)S(1)} %get-tuple-element.146), kind=kOutput, calls=%fused_computation.24.clone.1 | convolution fusion | flops 268468224 | bytes 8978496 | tf_op jit(solution)/shard_map/while/body/eval_jaxpr/dot_general | solution.py:39
  366.5 5.0 %fusion.56 = f32[32,4096]{1,0:T(8,128)S(1)} fusion(bf16[1024,4096]{1,0:T(8,128)(2,1)} %get-tuple-element.175, bf16[32,1024]{1,0:T(8,128)(2,1)S(1)} %get-tuple-element.161, bf16[32]{0:T(256)(128)(2,1)S(1)} %get-tuple-element.146), kind=kOutput, calls=%fused_computation.24.clone.1 | convolution fusion | flops 268468224 | bytes 8978496 | tf_op jit(solution)/shard_map/while/body/eval_jaxpr/dot_general | solution.py:39
  379.0 28.5 %all_to_all.20 = bf16[4,8,2,16,1024]{4,2,1,3,0:T(2,128)(2,1)S(1)} all-to-all(bf16[4,8,2,16,1024]{4,2,1,3,0:T(2,128)(2,1)S(1)} %pad_maximum_fusion), channel_id=1, replica_groups=mesh['batch'=32,'head'=4] {'head'}, dimensions={0} | all-to-all | bytes 4194304 | tf_op jit(solution)/shard_map/all_to_all | solution.py:94
  409.3 8.3 %maximum_convert_fusion = bf16[8,128,1024]{2,1,0:T(8,128)(2,1)S(1)} fusion(bf16[8,128,1024]{2,1,0:T(8,128)(2,1)S(1)} %bitcast.92, bf16[8,1024,1024]{2,1,0:T(8,128)(2,1)} %param.25), kind=kOutput, calls=%fused_computation.31 | convolution fusion | flops 2149580800 | bytes 20971520 | tf_op jit(solution)/shard_map/prh,phk->prk/dot_general | solution.py:104
  419.6 6.6 %all_to_all.21 = bf16[4,2,2304]{2,1,0:T(2,128)(2,1)S(1)} all-to-all(bf16[4,2,2304]{2,1,0:T(2,128)(2,1)S(1)} %reshape.124), channel_id=1, replica_groups=mesh['batch'=32,'head'=4] {'head'}, dimensions={0} | all-to-all | bytes 73728 | tf_op jit(solution)/shard_map/all_to_all | solution.py:115
  (167 shorter events, 112.9 us)
Async XLA Ops:
  7.2 410.4 %copy-start = (bf16[8,512,18]{1,0,2:T(8,128)(2,1)S(1)}, bf16[8,512,18]{1,0,2:T(8,128)(2,1)}, u32[]{:S(2)}) copy-start(bf16[8,512,18]{1,0,2:T(8,128)(2,1)} %param.27) | copy-start | bytes 442372
  7.2 10.6 %copy-start.1 = (bf16[32,24,512]{2,1,0:T(8,128)(2,1)S(1)}, bf16[32,24,512]{2,1,0:T(8,128)(2,1)}, u32[]{:S(2)}) copy-start(bf16[32,24,512]{2,1,0:T(8,128)(2,1)} %param.15) | copy-start | bytes 2359300
  7.2 10.9 %copy-start.10 = (s32[32]{0:T(128)S(1)}, s32[32]{0:T(128)}, u32[]{:S(2)}) copy-start(s32[32]{0:T(128)} %param.18) | copy-start | bytes 388
  7.2 10.9 %copy-start.8 = (s32[32,1]{0,1:T(1,128)S(1)}, s32[32,1]{0,1:T(1,128)}, u32[]{:S(2)}) copy-start(s32[32,1]{0,1:T(1,128)} %param.20) | copy-start | bytes 388
  7.2 11.1 %copy-start.6 = (s32[32,24]{0,1:T(8,128)S(1)}, s32[32,24]{0,1:T(8,128)}, u32[]{:S(2)}) copy-start(s32[32,24]{0,1:T(8,128)} %param.19) | copy-start | bytes 9220
  7.2 11.1 %copy-start.5 = (bf16[32,1024]{1,0:T(8,128)(2,1)S(1)}, bf16[32,1024]{1,0:T(8,128)(2,1)}, u32[]{:S(2)}) copy-start(bf16[32,1024]{1,0:T(8,128)(2,1)} %param.16) | copy-start | bytes 196612
  7.2 11.1 %copy-start.4 = (bf16[32,1024]{1,0:T(8,128)(2,1)S(1)}, bf16[32,1024]{1,0:T(8,128)(2,1)}, u32[]{:S(2)}) copy-start(bf16[32,1024]{1,0:T(8,128)(2,1)} %param.17) | copy-start | bytes 196612
  7.2 90.3 %all-gather.3.cloned.1.call-start = ((), (), s32[]{:S(2)}) async-start(), calls=%async_computation.2 | async-start | bytes 4325376 | tf_op jit(solution)/shard_map/all_gather | solution.py:73
  16.9 185.2 %all-gather.5.cloned.1.call-start = ((), (), s32[]{:S(2)}) async-start(), calls=%async_computation.3 | async-start | bytes 8650752 | tf_op jit(solution)/shard_map/all_gather | solution.py:77
  202.1 12.2 %copy-start.2 = (bf16[24,32,1024]{2,1,0:T(8,128)(2,1)S(1)}, bf16[24,32,1024]{2,1,0:T(8,128)(2,1)}, u32[]{:S(2)}) copy-start(bf16[24,32,1024]{2,1,0:T(8,128)(2,1)} %custom-call) | copy-start | bytes 4718596
  202.1 12.2 %copy-start.3 = (f32[4,1024]{1,0:T(4,128)S(1)}, f32[4,1024]{1,0:T(4,128)}, u32[]{:S(2)}) copy-start(f32[4,1024]{1,0:T(4,128)} %param.24) | copy-start | bytes 49156
  409.3 8.7 %copy-start.9 = (bf16[8,512]{1,0:T(8,128)(2,1)S(1)}, bf16[8,512]{1,0:T(8,128)(2,1)}, u32[]{:S(2)}) copy-start(bf16[8,512]{1,0:T(8,128)(2,1)} %param.26) | copy-start | bytes 24580
  418.0 9.2 %copy-start.7 = (s32[32,16]{0,1:T(8,128)S(1)}, s32[32,16]{0,1:T(8,128)}, u32[]{:S(2)}) copy-start(s32[32,16]{0,1:T(8,128)} %param.21) | copy-start | bytes 6148
Sparse Core Ops, SparseCore 0:
  17.0 80.4 all-gather.2
  100.6 101.4 all-gather.4
